TPU v7x, 8 devices: a whole 2x2x1 slice. The times are simulated.
8 devices in a mesh: dp: 2 (over z, y), sp: 4 (over x, core).
Axes of the slice: x: 2, y: 2, z: 1, core: 2. Of those that a mesh axis runs over, the one named last changes fastest.
Arguments:
- x: bfloat16 [64, 256, 256], P('dp', 'sp'), parts along dimension 0
- w_cur: bfloat16 [16, 8, 256, 512], replicated
- w_past: bfloat16 [16, 8, 256, 512], replicated
- w_res: bfloat16 [16, 8, 256, 256], replicated
- w_skip: bfloat16 [16, 8, 256, 256], replicated
Outputs:
- output 1: float32 [64, 4, 64, 256], P('dp', 'sp'), parts along dimension 0
- output 2: float32 [64, 4, 64, 256], P('dp', 'sp'), parts along dimension 0
There are 2 independent parts. A program takes and returns all parts, laid end to end along the dimension named above; an argument that names none is the same for every part.
All inputs are finite; a program needn't handle non-finite values.
Results may differ from a plain program's by a relative error of at most 0.00873732.
Values are sent between devices in bfloat16 or wider.
A program may use at most 1 GiB of HBM per device.

v0:
```python
import jax
import jax.numpy as jnp
from jax import lax
from jax.sharding import PartitionSpec as P


def solution(mesh):
    group_n = mesh.shape["sp"]

    def past_rows(u_cur, dilation):
        seq_dev = u_cur.shape[1]
        if dilation < seq_dev:
            halo_rows = lax.ppermute(u_cur[:, seq_dev - dilation:], "sp", [(source, source + 1) for source in range(group_n - 1)])
            return jnp.concatenate([halo_rows, u_cur[:, :seq_dev - dilation]], axis=1)
        hop_count = dilation // seq_dev
        return lax.ppermute(u_cur, "sp", [(source, source + hop_count) for source in range(group_n - hop_count)])

    def to_cyclic(local_rows):
        batch_n, seq_dev, feat_width = local_rows.shape
        grid_rows = local_rows.reshape(batch_n, seq_dev // group_n, group_n, feat_width)
        received = lax.all_to_all(grid_rows, "sp", 2, 1, tiled=True)
        return received.reshape(batch_n, 1, seq_dev, feat_width)

    def local_stack(x_loc, w_cur, w_past, w_res, w_skip):
        channels = x_loc.shape[-1]
        stacks, cycle_len = w_cur.shape[0], w_cur.shape[1]
        h_res = x_loc.astype(jnp.float32)
        skip_acc = jnp.zeros((x_loc.shape[0], x_loc.shape[1], w_skip.shape[-1]), jnp.float32)
        for stack_pos in range(stacks):
            for layer_pos in range(cycle_len):
                u_cur = h_res.astype(jnp.bfloat16)
                u_past = past_rows(u_cur, 2 ** layer_pos)
                pre_act = jnp.einsum("bsc,cd->bsd", u_cur, w_cur[stack_pos, layer_pos], preferred_element_type=jnp.float32) + jnp.einsum("bsc,cd->bsd", u_past, w_past[stack_pos, layer_pos], preferred_element_type=jnp.float32)
                gated = (jnp.tanh(pre_act[..., :channels]) * jax.nn.sigmoid(pre_act[..., channels:])).astype(jnp.bfloat16)
                h_res = h_res + jnp.einsum("bsc,cd->bsd", gated, w_res[stack_pos, layer_pos], preferred_element_type=jnp.float32)
                skip_acc = skip_acc + jnp.einsum("bsc,cd->bsd", gated, w_skip[stack_pos, layer_pos], preferred_element_type=jnp.float32)
        return to_cyclic(h_res), to_cyclic(skip_acc)

    return jax.shard_map(local_stack, mesh=mesh, in_specs=(P("dp", "sp", None), P(), P(), P(), P()), out_specs=(P("dp", "sp", None, None), P("dp", "sp", None, None)), check_vma=False)
```

profile of v0, /device:TPU:1, one launch (start us, length us, event | category | flops | bytes accessed | tf_op | source)
XLA Modules:
  0.0 1942.3 jit_solution(13622504611318454358)
XLA Ops:
  97.1 9.0 collective-permute-done.7
  111.7 8.1 collective-permute-start.8
  210.5 9.3 collective-permute-done.15
  225.3 8.1 collective-permute-start.16
  324.1 9.3 collective-permute-done.23
  437.9 9.1 collective-permute-done.31
  551.3 9.3 collective-permute-done.39
  566.2 8.1 collective-permute-start.40
  664.9 9.3 collective-permute-done.47
  778.8 9.0 collective-permute-done.55
  892.3 9.2 collective-permute-done.63
  1005.8 9.3 collective-permute-done.71
  1119.6 9.1 collective-permute-done.79
  1233.0 9.3 collective-permute-done.87
  1346.6 9.3 collective-permute-done.95
  1460.5 9.1 collective-permute-done.103
  1573.9 9.3 collective-permute-done.111
  1588.7 8.1 collective-permute-start.112
  1687.5 9.3 collective-permute-done.119
  1702.3 8.1 collective-permute-start.120
  1801.2 9.2 collective-permute-done.127
  1819.1 8.6 all-to-all-start
  1827.8 80.6 %add_add_fusion = f32[32,64,256]{2,1,0:T(8,128)} fusion(f32[32,64,256]{2,1,0:T(8,128)} %fusion.1569, f32[32,64,256]{2,1,0:T(8,128)} %fusion.1571, f32[32,64,256]{2,1,0:T(8,128)} %fusion.1573, f32[32,64,256]{2,1,0:T(8,128)} %fusion.1575, f32[32,64,256]{2,1,0:T(8,128)} %fusion.1577, f32[32,64,256]{2,1,0:T(8,128)} %fusion.1579, f32[32,64,256]{2,1,0:T(8,128)} %fusion.1581, ...), kind=kOutput, calls=%fused_computation.896 | convolution fusion | flops 335020032 | bytes 269615104 | tf_op jit(solution)/shard_map/bsc,cd->bsd/dot_general | solution.py:36
  1919.2 21.0 %all-to-all-done.1 = f32[32,16,4,256]{3,1,0,2:T(8,128)S(1)} async-done(((f32[32,16,4,256]{3,1,0,2:T(8,128)}), f32[32,16,4,256]{3,1,0,2:T(8,128)S(1)}, u32[]{:S(2)}, u32[]{:S(2)}) %all-to-all-start.1) | async-done | bytes 2097184 | tf_op jit(solution)/shard_map/all_to_all | solution.py:21
  (1014 shorter events, 1637.4 us)
Async XLA Ops:
  65.6 16.1 collective-permute-start.6
  85.6 20.5 %collective-permute-start.7 = (bf16[32,64,256]{2,1,0:T(8,128)(2,1)S(1)}, bf16[32,64,256]{2,1,0:T(8,128)(2,1)S(1)}, u32[]{:S(2)}, u32[]{:S(2)}) collective-permute-start(bf16[32,64,256]{2,1,0:T(8,128)(2,1)S(1)} %get-tuple-element.48), channel_id=1, source_target_pairs={{0,2},{1,3},{4,6},{5,7}} | collective-permute-start | bytes 3145736 | tf_op jit(solution)/shard_map/ppermute | solution.py:16
  179.3 16.1 collective-permute-start.14
  199.2 20.6 %collective-permute-start.15 = (bf16[32,64,256]{2,1,0:T(8,128)(2,1)S(1)}, bf16[32,64,256]{2,1,0:T(8,128)(2,1)S(1)}, u32[]{:S(2)}, u32[]{:S(2)}) collective-permute-start(bf16[32,64,256]{2,1,0:T(8,128)(2,1)S(1)} %get-tuple-element.64), channel_id=1, source_target_pairs={{0,2},{1,3},{4,6},{5,7}} | collective-permute-start | bytes 3145736 | tf_op jit(solution)/shard_map/ppermute | solution.py:16
  312.8 20.6 %collective-permute-start.23 = (bf16[32,64,256]{2,1,0:T(8,128)(2,1)S(1)}, bf16[32,64,256]{2,1,0:T(8,128)(2,1)S(1)}, u32[]{:S(2)}, u32[]{:S(2)}) collective-permute-start(bf16[32,64,256]{2,1,0:T(8,128)(2,1)S(1)} %get-tuple-element.80), channel_id=1, source_target_pairs={{0,2},{1,3},{4,6},{5,7}} | collective-permute-start | bytes 3145736 | tf_op jit(solution)/shard_map/ppermute | solution.py:16
  406.5 16.1 collective-permute-start.30
  426.4 20.6 %collective-permute-start.31 = (bf16[32,64,256]{2,1,0:T(8,128)(2,1)S(1)}, bf16[32,64,256]{2,1,0:T(8,128)(2,1)S(1)}, u32[]{:S(2)}, u32[]{:S(2)}) collective-permute-start(bf16[32,64,256]{2,1,0:T(8,128)(2,1)S(1)} %get-tuple-element.96), channel_id=1, source_target_pairs={{0,2},{1,3},{4,6},{5,7}} | collective-permute-start | bytes 3145736 | tf_op jit(solution)/shard_map/ppermute | solution.py:16
  520.1 16.1 collective-permute-start.38
  540.1 20.6 %collective-permute-start.39 = (bf16[32,64,256]{2,1,0:T(8,128)(2,1)S(1)}, bf16[32,64,256]{2,1,0:T(8,128)(2,1)S(1)}, u32[]{:S(2)}, u32[]{:S(2)}) collective-permute-start(bf16[32,64,256]{2,1,0:T(8,128)(2,1)S(1)} %get-tuple-element.112), channel_id=1, source_target_pairs={{0,2},{1,3},{4,6},{5,7}} | collective-permute-start | bytes 3145736 | tf_op jit(solution)/shard_map/ppermute | solution.py:16
  633.7 16.1 collective-permute-start.46
  653.7 20.6 %collective-permute-start.47 = (bf16[32,64,256]{2,1,0:T(8,128)(2,1)S(1)}, bf16[32,64,256]{2,1,0:T(8,128)(2,1)S(1)}, u32[]{:S(2)}, u32[]{:S(2)}) collective-permute-start(bf16[32,64,256]{2,1,0:T(8,128)(2,1)S(1)} %get-tuple-element.128), channel_id=1, source_target_pairs={{0,2},{1,3},{4,6},{5,7}} | collective-permute-start | bytes 3145736 | tf_op jit(solution)/shard_map/ppermute | solution.py:16
  747.4 16.1 collective-permute-start.54
  767.3 20.6 %collective-permute-start.55 = (bf16[32,64,256]{2,1,0:T(8,128)(2,1)S(1)}, bf16[32,64,256]{2,1,0:T(8,128)(2,1)S(1)}, u32[]{:S(2)}, u32[]{:S(2)}) collective-permute-start(bf16[32,64,256]{2,1,0:T(8,128)(2,1)S(1)} %get-tuple-element.144), channel_id=1, source_target_pairs={{0,2},{1,3},{4,6},{5,7}} | collective-permute-start | bytes 3145736 | tf_op jit(solution)/shard_map/ppermute | solution.py:16
  880.9 20.6 %collective-permute-start.63 = (bf16[32,64,256]{2,1,0:T(8,128)(2,1)S(1)}, bf16[32,64,256]{2,1,0:T(8,128)(2,1)S(1)}, u32[]{:S(2)}, u32[]{:S(2)}) collective-permute-start(bf16[32,64,256]{2,1,0:T(8,128)(2,1)S(1)} %get-tuple-element.160), channel_id=1, source_target_pairs={{0,2},{1,3},{4,6},{5,7}} | collective-permute-start | bytes 3145736 | tf_op jit(solution)/shard_map/ppermute | solution.py:16
  994.5 20.6 %collective-permute-start.71 = (bf16[32,64,256]{2,1,0:T(8,128)(2,1)S(1)}, bf16[32,64,256]{2,1,0:T(8,128)(2,1)S(1)}, u32[]{:S(2)}, u32[]{:S(2)}) collective-permute-start(bf16[32,64,256]{2,1,0:T(8,128)(2,1)S(1)} %get-tuple-element.176), channel_id=1, source_target_pairs={{0,2},{1,3},{4,6},{5,7}} | collective-permute-start | bytes 3145736 | tf_op jit(solution)/shard_map/ppermute | solution.py:16
  1108.1 20.6 %collective-permute-start.79 = (bf16[32,64,256]{2,1,0:T(8,128)(2,1)S(1)}, bf16[32,64,256]{2,1,0:T(8,128)(2,1)S(1)}, u32[]{:S(2)}, u32[]{:S(2)}) collective-permute-start(bf16[32,64,256]{2,1,0:T(8,128)(2,1)S(1)} %get-tuple-element.192), channel_id=1, source_target_pairs={{0,2},{1,3},{4,6},{5,7}} | collective-permute-start | bytes 3145736 | tf_op jit(solution)/shard_map/ppermute | solution.py:16
  1221.8 20.6 %collective-permute-start.87 = (bf16[32,64,256]{2,1,0:T(8,128)(2,1)S(1)}, bf16[32,64,256]{2,1,0:T(8,128)(2,1)S(1)}, u32[]{:S(2)}, u32[]{:S(2)}) collective-permute-start(bf16[32,64,256]{2,1,0:T(8,128)(2,1)S(1)} %get-tuple-element.208), channel_id=1, source_target_pairs={{0,2},{1,3},{4,6},{5,7}} | collective-permute-start | bytes 3145736 | tf_op jit(solution)/shard_map/ppermute | solution.py:16
  1335.4 20.6 %collective-permute-start.95 = (bf16[32,64,256]{2,1,0:T(8,128)(2,1)S(1)}, bf16[32,64,256]{2,1,0:T(8,128)(2,1)S(1)}, u32[]{:S(2)}, u32[]{:S(2)}) collective-permute-start(bf16[32,64,256]{2,1,0:T(8,128)(2,1)S(1)} %get-tuple-element.224), channel_id=1, source_target_pairs={{0,2},{1,3},{4,6},{5,7}} | collective-permute-start | bytes 3145736 | tf_op jit(solution)/shard_map/ppermute | solution.py:16
  1449.0 20.6 %collective-permute-start.103 = (bf16[32,64,256]{2,1,0:T(8,128)(2,1)S(1)}, bf16[32,64,256]{2,1,0:T(8,128)(2,1)S(1)}, u32[]{:S(2)}, u32[]{:S(2)}) collective-permute-start(bf16[32,64,256]{2,1,0:T(8,128)(2,1)S(1)} %get-tuple-element.240), channel_id=1, source_target_pairs={{0,2},{1,3},{4,6},{5,7}} | collective-permute-start | bytes 3145736 | tf_op jit(solution)/shard_map/ppermute | solution.py:16
  1562.6 20.6 %collective-permute-start.111 = (bf16[32,64,256]{2,1,0:T(8,128)(2,1)S(1)}, bf16[32,64,256]{2,1,0:T(8,128)(2,1)S(1)}, u32[]{:S(2)}, u32[]{:S(2)}) collective-permute-start(bf16[32,64,256]{2,1,0:T(8,128)(2,1)S(1)} %get-tuple-element.256), channel_id=1, source_target_pairs={{0,2},{1,3},{4,6},{5,7}} | collective-permute-start | bytes 3145736 | tf_op jit(solution)/shard_map/ppermute | solution.py:16
  1676.2 20.6 %collective-permute-start.119 = (bf16[32,64,256]{2,1,0:T(8,128)(2,1)S(1)}, bf16[32,64,256]{2,1,0:T(8,128)(2,1)S(1)}, u32[]{:S(2)}, u32[]{:S(2)}) collective-permute-start(bf16[32,64,256]{2,1,0:T(8,128)(2,1)S(1)} %get-tuple-element.272), channel_id=1, source_target_pairs={{0,2},{1,3},{4,6},{5,7}} | collective-permute-start | bytes 3145736 | tf_op jit(solution)/shard_map/ppermute | solution.py:16
  1789.8 20.6 %collective-permute-start.127 = (bf16[32,64,256]{2,1,0:T(8,128)(2,1)S(1)}, bf16[32,64,256]{2,1,0:T(8,128)(2,1)S(1)}, u32[]{:S(2)}, u32[]{:S(2)}) collective-permute-start(bf16[32,64,256]{2,1,0:T(8,128)(2,1)S(1)} %get-tuple-element.288), channel_id=1, source_target_pairs={{0,2},{1,3},{4,6},{5,7}} | collective-permute-start | bytes 3145736 | tf_op jit(solution)/shard_map/ppermute | solution.py:16
  1819.1 92.8 %all-to-all-start = ((f32[32,16,4,256]{3,1,0,2:T(8,128)}), f32[32,16,4,256]{3,1,0,2:T(8,128)}, u32[]{:S(2)}, u32[]{:S(2)}) async-start(f32[32,16,4,256]{3,1,0,2:T(8,128)} %copy.11), calls=%async_computation | async-start | bytes 4194304 | tf_op jit(solution)/shard_map/all_to_all | solution.py:21
  1912.0 28.3 %all-to-all-start.1 = ((f32[32,16,4,256]{3,1,0,2:T(8,128)}), f32[32,16,4,256]{3,1,0,2:T(8,128)S(1)}, u32[]{:S(2)}, u32[]{:S(2)}) async-start(f32[32,16,4,256]{3,1,0,2:T(8,128)} %copy.13), calls=%async_computation.1 | async-start | bytes 4194304 | tf_op jit(solution)/shard_map/all_to_all | solution.py:21
  (108 other events, 880.2 us)
where the time goes:
time: 1970 us; the launch traced here: 1940 us
  matrix products  1020 us (52%)
  starting transfers between devices  539 us (27%)
  waiting for transfers between devices  255 us (13%)
  other arithmetic  105 us (5%)
    ppermute x96, starting transfers between devices, past_rows(): lax.ppermute(u_cur[:, seq_dev - dilation:], 'sp', [(source, source + 1) f...  430 us
    dot_general x128, matrix products, local_stack(): jnp.einsum('bsc,cd->bsd', gated, w_skip[stack_pos, layer_pos], preferred_...  421 us
    dot_general x128, matrix products, local_stack(): jnp.einsum('bsc,cd->bsd', u_past, w_past[stack_pos, layer_pos], preferred...  212 us
    dot_general x128, matrix products, local_stack(): jnp.einsum('bsc,cd->bsd', u_cur, w_cur[stack_pos, layer_pos], preferred_e...  211 us
    ppermute x32, waiting for transfers between devices, past_rows(): lax.ppermute(u_cur, 'sp', [(source, source + hop_count) for source in ran...  180 us
    dot_general x128, matrix products, local_stack(): jnp.einsum('bsc,cd->bsd', gated, w_res[stack_pos, layer_pos], preferred_e...  173 us
    convert_element_type x128, other arithmetic, local_stack(): (jnp.tanh(pre_act[..., :channels]) * jax.nn.sigmoid(pre_act[..., channels...  105 us
    ppermute x32, starting transfers between devices, past_rows(): lax.ppermute(u_cur, 'sp', [(source, source + hop_count) for source in ran...  96.2 us
  transfers between devices with their start and end apart: 130, of which 66 were waited for; matrix products, arithmetic and copies ran while one was open for 32% of the time, Pallas kernels for 0%

commit v1 on v0

v1 whole, which is shorter than its diff:
```python
import jax
import jax.numpy as jnp
from jax import lax
from jax.experimental import pallas as pl
from jax.experimental.pallas import tpu as pltpu
from jax.sharding import PartitionSpec as P

F32, BF16 = jnp.float32, jnp.bfloat16

HEAD = 1
TAIL = 4
SLOTS = TAIL + 1
M_WIDE = 512
M_BLK = 128
LAG_WIDE = 1
LAG_BLK = 1


def solution(mesh):
    G = mesh.shape["sp"]

    def kernel(x, wc, wp, wr, ws, ho, so, h, sk, u, bc, bp, br, bs, b1, b2, b3, b4, b5, b6, b7, e8, xb, st, wsem, xsend, xrecv, xloc, osend, orecv, oloc):
        batch, seq_blk, C = x.shape
        S, L = wc.shape[0], wc.shape[1]
        NB = batch // G
        RB = seq_blk * NB
        R = RB * G
        PAD = u.shape[1] - R
        OL = seq_blk // G
        me = lax.axis_index("sp")
        hist = {1: b1, 2: b2, 3: b3, 4: b4, 5: b5, 6: b6, 7: b7}

        def rows(ref, r, m, stride=None):
            return jnp.concatenate([ref[k, pl.ds(r, m, stride=stride), :] for k in range(2)], axis=1)

        def put(ref, r, m, v, stride=None):
            for k in range(2):
                ref[k, pl.ds(r, m, stride=stride), :] = v[:, k * C // 2:(k + 1) * C // 2]

        def weights(s, slot):
            pairs = ((wc, bc), (wp, bp), (wr, br), (ws, bs))
            return [pltpu.make_async_copy(src.at[s], dst.at[slot], wsem.at[slot, k]) for k, (src, dst) in enumerate(pairs)]

        def start_weights(s):
            for c in weights(s, lax.rem(s, SLOTS)):
                c.start()

        def wait_weights(s):
            for c in weights(s, lax.rem(s, SLOTS)):
                c.wait()

        def x_remote(o, src):
            peer = lax.rem(me + o, G)
            return pltpu.make_async_remote_copy(
                src_ref=x.at[pl.ds(peer * NB, NB)], dst_ref=xb.at[src], send_sem=xsend.at[o], recv_sem=xrecv.at[src],
                device_id={"sp": peer}, device_id_type=pl.DeviceIdType.MESH)

        def x_local():
            return pltpu.make_async_copy(x.at[pl.ds(me * NB, NB)], xb.at[me], xloc)

        def out_remote(b, q, o, src):
            peer = lax.rem(me + o, G)
            dst = (ho, so)[q]
            return pltpu.make_async_remote_copy(
                src_ref=st.at[b, q, peer], dst_ref=dst.at[pl.ds(src * NB, NB), 0, pl.ds(OL * b, OL), :],
                send_sem=osend.at[b, q, o], recv_sem=orecv.at[b, q, src],
                device_id={"sp": peer}, device_id_type=pl.DeviceIdType.MESH)

        def out_local(b, q):
            dst = (ho, so)[q]
            return pltpu.make_async_copy(st.at[b, q, me], dst.at[pl.ds(me * NB, NB), 0, pl.ds(OL * b, OL), :], oloc.at[b, q])

        for s in range(SLOTS):
            start_weights(s)
        barrier = pltpu.get_barrier_semaphore()
        for o in range(1, G):
            pl.semaphore_signal(barrier, inc=1, device_id={"sp": lax.rem(me + o, G)}, device_id_type=pl.DeviceIdType.MESH)
        x_local().start()
        pl.semaphore_wait(barrier, G - 1)
        for o in range(1, G):
            x_remote(o, me).start()

        u[:, pl.ds(0, PAD), :] = jnp.zeros((2, PAD, C), BF16)
        put(h, 0, NB, jnp.zeros((NB, C), F32))

        def load_block(b):
            @pl.when(me == b)
            def _():
                x_local().wait()

            @pl.when(me != b)
            def _():
                x_remote(1, b).wait_recv()

            for bb in range(NB):
                put(h, NB + RB * b + bb, seq_blk, xb[b, bb].astype(F32), stride=NB)
            u[0, pl.ds(PAD + RB * b, RB), :] = rows(h, NB + RB * b, RB).astype(BF16)
            put(sk, RB * b, RB, jnp.zeros((RB, C), F32))

        def send_block(b):
            for q in range(2):
                src, base = ((h, NB), (sk, 0))[q]
                for j in range(G):
                    for bb in range(NB):
                        st[b, q, j, bb] = rows(src, base + RB * b + NB * j + bb, OL, stride=NB * G)
            for o in range(1, G):
                for q in range(2):
                    out_remote(b, q, o, me).start()
            for q in range(2):
                out_local(b, q).start()

        def pipeline(tasks, lag, g1, g2):
            zs = {}
            for k in range(len(tasks) + lag):
                if k < len(tasks):
                    zs[tasks[k]] = g1(*tasks[k])
                if k >= lag:
                    g2(*tasks[k - lag], zs.pop(tasks[k - lag]))

        def preact(cur, past, slot, i):
            z = jnp.dot(cur, bc[slot, i], preferred_element_type=F32)
            if past is not None:
                z = z + jnp.dot(past, bp[slot, i], preferred_element_type=F32)
            return z

        def update(z, slot, i, r0, m):
            a = (jnp.tanh(z[:, :C]) * jax.nn.sigmoid(z[:, C:])).astype(BF16)
            hn = rows(h, NB + r0, m) + jnp.dot(a, br[slot, i], preferred_element_type=F32)
            put(h, NB + r0, m, hn)
            put(sk, r0, m, rows(sk, r0, m) + jnp.dot(a, bs[slot, i], preferred_element_type=F32))
            return hn.astype(BF16)

        def wide_stack(s, carry):
            slot = lax.rem(s, SLOTS)
            wait_weights(s)

            @pl.when(s == HEAD)
            def _():
                for k in range(HEAD):
                    start_weights(k + SLOTS)

            @pl.when((s > HEAD) & (s - 1 + SLOTS < S))
            def _():
                start_weights(s - 1 + SLOTS)

            def g1(i, c):
                off, r0 = NB << i, c * M_WIDE
                past = None
                if r0 + M_WIDE > off:
                    if i == 0:
                        past = rows(h, NB + r0 - off, M_WIDE).astype(BF16)
                    else:
                        past = u[i % 2, pl.ds(PAD + r0 - off, M_WIDE), :]
                return preact(u[i % 2, pl.ds(PAD + r0, M_WIDE), :], past, slot, i)

            def g2(i, c, z):
                r0 = c * M_WIDE
                u[(i + 1) % 2, pl.ds(PAD + r0, M_WIDE), :] = update(z, slot, i, r0, M_WIDE)

            pipeline([(i, c) for i in range(L) for c in range(R // M_WIDE)], LAG_WIDE, g1, g2)
            return carry

        def block_stack(b, s, k):
            slot = lax.rem(s, SLOTS)
            if b == 0:
                wait_weights(s)
            last = RB // M_BLK - 1

            def place(i):
                off = NB << i
                return off if off < RB else RB * b

            def g1(i, c):
                off, r0 = NB << i, RB * b + c * M_BLK
                past = None
                if i == 0:
                    cur = u[0, pl.ds(PAD + r0, M_BLK), :]
                    if c == 0:
                        first = jnp.zeros((NB, C), F32) if b == 0 else e8[k]
                        past = jnp.concatenate([first, rows(h, NB + r0, M_BLK - NB)], axis=0).astype(BF16)
                    else:
                        past = rows(h, r0, M_BLK).astype(BF16)
                    if c == last and b < G - 1:
                        e8[k] = rows(h, r0 + M_BLK, NB)
                else:
                    buf = hist[i]
                    cur = buf[k, pl.ds(place(i) + c * M_BLK, M_BLK), :]
                    if b == 0 and c == 0 and off < RB:
                        buf[k, pl.ds(0, off), :] = jnp.zeros((off, C), BF16)
                    if r0 + M_BLK > off:
                        past = buf[k, pl.ds(place(i) + c * M_BLK - off, M_BLK), :]
                    if c == last and b < G - 1 and off < RB:
                        buf[k, pl.ds(0, off), :] = buf[k, pl.ds(RB, off), :]
                return preact(cur, past, slot, i)

            def g2(i, c, z):
                r0 = RB * b + c * M_BLK
                un = update(z, slot, i, r0, M_BLK)
                if i == L - 1:
                    u[0, pl.ds(PAD + r0, M_BLK), :] = un
                else:
                    hist[i + 1][k, pl.ds(place(i + 1) + c * M_BLK, M_BLK), :] = un

            pipeline([(i, c) for i in range(L) for c in range(last + 1)], LAG_BLK, g1, g2)

        def phase(p, carry):
            lo = p * (S - TAIL)
            n = jnp.where(p == 0, HEAD, TAIL)
            for b in range(G):
                @pl.when(p == 0)
                def _():
                    load_block(b)

                def step(k, carry):
                    block_stack(b, lo + k, k)
                    return carry

                lax.fori_loop(0, n, step, 0)

                @pl.when(p == 1)
                def _():
                    send_block(b)

            lax.fori_loop(HEAD, jnp.where(p == 0, S - TAIL, HEAD), wide_stack, 0)
            return carry

        lax.fori_loop(0, 2, phase, 0)

        for o in range(1, G):
            x_remote(o, me).wait_send()
        for b in range(G):
            for q in range(2):
                out_local(b, q).wait()
                for o in range(1, G):
                    out_remote(b, q, o, me).wait_send()
                    out_remote(b, q, o, lax.rem(me + G - o, G)).wait_recv()

    def local(x, wc, wp, wr, ws):
        batch, seq_blk, C = x.shape
        S, L = wc.shape[0], wc.shape[1]
        NB = batch // G
        RB = seq_blk * NB
        R = RB * G
        KB = max(HEAD, TAIL)
        hist = [pltpu.VMEM((KB, (NB << i) + RB if (NB << i) < RB else R, C), BF16) for i in range(1, L)]
        hbm = pl.BlockSpec(memory_space=pltpu.HBM)
        out = jax.ShapeDtypeStruct((batch, 1, seq_blk, C), F32)
        return pl.pallas_call(
            kernel,
            out_shape=[out, out],
            in_specs=[hbm] * 5,
            out_specs=[hbm] * 2,
            scratch_shapes=[
                pltpu.VMEM((2, R + NB, C // 2), F32),
                pltpu.VMEM((2, R, C // 2), F32),
                pltpu.VMEM((2, R + M_WIDE // 2, C), BF16),
                pltpu.VMEM((SLOTS, L, C, 2 * C), BF16),
                pltpu.VMEM((SLOTS, L, C, 2 * C), BF16),
                pltpu.VMEM((SLOTS, L, C, C), BF16),
                pltpu.VMEM((SLOTS, L, C, C), BF16),
                *hist,
                pltpu.VMEM((KB, NB, C), F32),
                pltpu.VMEM((G, NB, seq_blk, C), BF16),
                pltpu.VMEM((G, 2, G, NB, seq_blk // G, C), F32),
                pltpu.SemaphoreType.DMA((SLOTS, 4)),
                pltpu.SemaphoreType.DMA((G,)),
                pltpu.SemaphoreType.DMA((G,)),
                pltpu.SemaphoreType.DMA,
                pltpu.SemaphoreType.DMA((G, 2, G)),
                pltpu.SemaphoreType.DMA((G, 2, G)),
                pltpu.SemaphoreType.DMA((G, 2)),
            ],
            compiler_params=pltpu.CompilerParams(collective_id=0, has_side_effects=True, vmem_limit_bytes=67000000),
            name="stack",
        )(x, wc, wp, wr, ws)

    return jax.shard_map(local, mesh=mesh, in_specs=(P("dp", "sp", None), P(), P(), P(), P()), out_specs=(P("dp", "sp", None, None), P("dp", "sp", None, None)), check_vma=False)
```

time: 1970 us -> 251 us (0.13); the launches traced: 1940 us -> 251 us
  matrix products: 1020 us -> 0 us
  starting transfers between devices: 539 us -> 0 us
  waiting for transfers between devices: 255 us -> 0 us
  Pallas kernels: 0 us -> 244 us
  other arithmetic: 105 us -> 0 us
    dot_general x512 -> x0, matrix products: 1020 us -> none  [the longest x128 421 us: local_stack(): jnp.einsum('bsc,cd->bsd', gated, w_skip[stack_pos, layer_pos], preferred_...]
    ppermute x128 -> x0, starting transfers between devices: 526 us -> none  [the longest x96 430 us: past_rows(): lax.ppermute(u_cur[:, seq_dev - dilation:], 'sp', [(source, source + 1) f...]
    pallas_call x0 -> x1, Pallas kernels: none -> 244 us  [local(): pl.pallas_call(kernel, out_shape=[out, out], in_specs=[hbm] * 5, out_spec...]
    ppermute x128 -> x0, waiting for transfers between devices: 234 us -> none  [the longest x32 180 us: past_rows(): lax.ppermute(u_cur, 'sp', [(source, source + hop_count) for source in ran...]
    convert_element_type x128 -> x0, other arithmetic: 105 us -> none  [local_stack(): (jnp.tanh(pre_act[..., :channels]) * jax.nn.sigmoid(pre_act[..., channels...]
    all_to_all x2 -> x0, waiting for transfers between devices: 21 us -> none  [to_cyclic(): received = lax.all_to_all(grid_rows, 'sp', 2, 1, tiled=True)]
  transfers between devices with their start and end apart: 130 -> 0, of which waited for: 66 -> 0; matrix products, arithmetic and copies ran while one was open for 32% -> 0% of each run, Pallas kernels for 0% -> 0%
where the time goes in v1:
time: 251 us
  Pallas kernels  244 us (97%)
  local copies, waits for them, and re-layouts  6.26 us (2%)
    pallas_call x1, Pallas kernels, local(): pl.pallas_call(kernel, out_shape=[out, out], in_specs=[hbm] * 5, out_spec...  244 us
    unnamed x2, local copies, waits for them, and re-layouts  6.26 us

profile of v1, /device:TPU:1, one launch (start us, length us, event | category | flops | bytes accessed | tf_op | source)
XLA Modules:
  0.0 250.6 jit_solution(3823120005469083766)
XLA Ops:
  0.6 243.7 %stack.1 = (f32[32,1,64,256]{3,2,1,0:T(8,128)}, f32[32,1,64,256]{3,2,1,0:T(8,128)}) custom-call(bf16[32,64,256]{2,1,0:T(8,128)(2,1)} %x.1, bf16[16,8,256,512]{3,2,1,0:T(8,128)(2,1)} %wc.1, bf16[16,8,256,512]{3,2,1,0:T(8,128)(2,1)} %wp.1, bf16[16,8,256,256]{3,2,1,0:T(8,128)(2,1)} %wr.1, bf16[16,8,256,256]{3,2,1,0:T(8,128)(2,1)} %ws.1), custom_call_target="tpu_custom_call" | custom-call | tf_op jit(solution)/shard_map/stack/pallas_call | solution.py:248
  244.3 3.1 %copy.9 = f32[32,1,64,256]{3,2,1,0:T(8,128)} copy(f32[32,1,64,256]{3,2,1,0:T(8,128)} %get-tuple-element.4) | data formatting | bytes 4194304
  247.4 3.1 %copy.10 = f32[32,1,64,256]{3,2,1,0:T(8,128)} copy(f32[32,1,64,256]{3,2,1,0:T(8,128)} %get-tuple-element.5) | data formatting | bytes 4194304

commit v2 on v1

v2 whole, which is shorter than its diff:
```python
import jax
import jax.numpy as jnp
from jax import lax
from jax.experimental import pallas as pl
from jax.experimental.pallas import tpu as pltpu
from jax.sharding import PartitionSpec as P

F32, BF16 = jnp.float32, jnp.bfloat16

TAIL = 3
SLOTS = 4
M_WIDE = 512
M_BLK = 128
VMEM = 48 << 20


def solution(mesh):
    G = mesh.shape["sp"]

    def kernel(x, wc, wp, wr, ws, ho, so, h, sk, u, bc, bp, br, bs, b1, b2, b3, b4, b5, b6, b7, e8, hb, skb, ub, xb, st, wsem, xsend, xrecv, xloc, osend, orecv, oloc):
        batch, seq_blk, C = x.shape
        S, L = wc.shape[0], wc.shape[1]
        NB = batch // G
        RB = seq_blk * NB
        R = RB * G
        PAD = u.shape[1] - R
        OL = seq_blk // G
        me = lax.axis_index("sp")
        hist = {1: b1, 2: b2, 3: b3, 4: b4, 5: b5, 6: b6, 7: b7}

        def rows(ref, r, m, stride=None):
            return jnp.concatenate([ref[k, pl.ds(r, m, stride=stride), :] for k in range(2)], axis=1)

        def put(ref, r, m, v, stride=None):
            for k in range(2):
                ref[k, pl.ds(r, m, stride=stride), :] = v[:, k * C // 2:(k + 1) * C // 2]

        def weights(s, slot):
            pairs = ((wc, bc), (wp, bp), (wr, br), (ws, bs))
            return [pltpu.make_async_copy(src.at[s], dst.at[slot], wsem.at[slot, k]) for k, (src, dst) in enumerate(pairs)]

        def start_weights(s):
            for c in weights(s, lax.rem(s, SLOTS)):
                c.start()

        def wait_weights(s):
            for c in weights(s, lax.rem(s, SLOTS)):
                c.wait()

        def x_remote(o, src):
            peer = lax.rem(me + o, G)
            return pltpu.make_async_remote_copy(
                src_ref=x.at[pl.ds(peer * NB, NB)], dst_ref=xb.at[src], send_sem=xsend.at[o], recv_sem=xrecv.at[src],
                device_id={"sp": peer}, device_id_type=pl.DeviceIdType.MESH)

        def x_local():
            return pltpu.make_async_copy(x.at[pl.ds(me * NB, NB)], xb.at[me], xloc)

        def out_remote(b, q, o, src):
            peer = lax.rem(me + o, G)
            dst = (ho, so)[q]
            return pltpu.make_async_remote_copy(
                src_ref=st.at[lax.rem(b, 2), q, peer], dst_ref=dst.at[pl.ds(src * NB, NB), 0, pl.ds(OL * b, OL), :],
                send_sem=osend.at[b, q, o], recv_sem=orecv.at[b, q, src],
                device_id={"sp": peer}, device_id_type=pl.DeviceIdType.MESH)

        def out_local(b, q):
            dst = (ho, so)[q]
            return pltpu.make_async_copy(st.at[lax.rem(b, 2), q, me], dst.at[pl.ds(me * NB, NB), 0, pl.ds(OL * b, OL), :], oloc.at[b, q])

        for s in range(1):
            start_weights(s)
        barrier = pltpu.get_barrier_semaphore()
        for o in range(1, G):
            pl.semaphore_signal(barrier, inc=1, device_id={"sp": lax.rem(me + o, G)}, device_id_type=pl.DeviceIdType.MESH)
        x_local().start()
        pl.semaphore_wait(barrier, G - 1)
        odd = lax.rem(me, 2) == 1
        x_near = [lax.rem(me, 2) * (G - 2) + 1, G // 2, G - 1 - lax.rem(me, 2) * (G - 2)]

        def send_x_far():
            x_remote(x_near[1], me).start()
            x_remote(x_near[2], me).start()

        @pl.when(jnp.logical_not(odd))
        def _():
            send_x_far()

        x_remote(x_near[0], me).start()

        u[:, pl.ds(0, PAD), :] = jnp.zeros((2, PAD, C), BF16)
        put(h, 0, NB, jnp.zeros((NB, C), F32))

        def load_block(b):
            @pl.when(me == b)
            def _():
                x_local().wait()

            @pl.when(me != b)
            def _():
                x_remote(1, b).wait_recv()

            for bb in range(NB):
                put(hb, bb, seq_blk, xb[b, bb].astype(F32), stride=NB)
            ub[...] = rows(hb, 0, RB).astype(BF16)
            skb[...] = jnp.zeros_like(skb)

        def block_views(b):
            r0 = pl.multiple_of(RB * b, RB)
            return ((hb, h.at[:, pl.ds(pl.multiple_of(r0 + NB, NB), RB), :]), (skb, sk.at[:, pl.ds(r0, RB), :]),
                    (ub, u.at[0, pl.ds(pl.multiple_of(PAD + r0, M_BLK), RB), :]))

        def fetch_block(b):
            for small, full in block_views(b):
                small[...] = full[...]

        def store_block(b):
            for small, full in block_views(b):
                full[...] = small[...]

        def sent(b):
            for q in range(2):
                out_local(b, q).wait()
                for o in range(1, G):
                    out_remote(b, q, o, me).wait_send()

        def send_block(b):
            @pl.when(b >= 2)
            def _():
                sent(b - 2)

            for q in range(2):
                src = (hb, skb)[q]
                for j in range(G):
                    for bb in range(NB):
                        st[lax.rem(b, 2), q, j, bb] = rows(src, NB * j + bb, OL, stride=NB * G)
            for o in range(1, G):
                for q in range(2):
                    out_remote(b, q, o, me).start()
            for q in range(2):
                out_local(b, q).start()

        def wide_order(n):
            tasks = [(i, c) for i in range(L) for c in range(n)]
            for prev, cur in zip([None] + tasks, tasks + [None]):
                if cur:
                    yield 1, *cur
                if prev:
                    yield 2, *prev

        def block_order(n):
            for i in range(n):
                yield 1, i, 0
                if i:
                    yield 2, i - 1, 3
                for half, c in ((1, 1), (1, 2), (2, 0), (1, 3), (2, 1), (2, 2)):
                    yield half, i, c
            yield 2, n - 1, 3

        def pipeline(order, g1, g2):
            zs = {}
            for half, i, c in order:
                if half == 1:
                    zs[i, c] = g1(i, c)
                else:
                    g2(i, c, zs.pop((i, c)))

        def preact(cur, past, slot, i):
            z = jnp.dot(cur, bc[slot, i], preferred_element_type=F32)
            if past is not None:
                z = z + jnp.dot(past, bp[slot, i], preferred_element_type=F32)
            return z

        def update(z, slot, i, r0, m, h=h, sk=sk, pad=None):
            pad = NB if pad is None else pad
            a = (jnp.tanh(z[:, :C]) * jax.nn.sigmoid(z[:, C:])).astype(BF16)
            hn = rows(h, r0 + pad, m) + jnp.dot(a, br[slot, i], preferred_element_type=F32)
            put(h, r0 + pad, m, hn)
            put(sk, r0, m, rows(sk, r0, m) + jnp.dot(a, bs[slot, i], preferred_element_type=F32))
            return hn.astype(BF16)

        def wide_stack(s, carry):
            slot = lax.rem(s, SLOTS)
            wait_weights(s)

            @pl.when(s - 1 + SLOTS < S)
            def _():
                start_weights(s - 1 + SLOTS)

            def g1(i, c):
                off, r0 = NB << i, c * M_WIDE
                past = None
                if r0 + M_WIDE > off:
                    if i == 0:
                        past = rows(h, NB + r0 - off, M_WIDE).astype(BF16)
                    else:
                        past = u[i % 2, pl.ds(PAD + r0 - off, M_WIDE), :]
                return preact(u[i % 2, pl.ds(PAD + r0, M_WIDE), :], past, slot, i)

            def g2(i, c, z):
                r0 = c * M_WIDE
                u[(i + 1) % 2, pl.ds(PAD + r0, M_WIDE), :] = update(z, slot, i, r0, M_WIDE)

            pipeline(wide_order(R // M_WIDE), g1, g2)
            return carry

        def clear_history():
            e8[...] = jnp.zeros_like(e8)
            for i, buf in hist.items():
                for k in range(TAIL):
                    buf[k, pl.ds(0, NB << i), :] = jnp.zeros((NB << i, C), BF16)

        def block_stacks(s0, count):
            last = RB // M_BLK - 1

            def g1(n, c):
                k, i = n // L, n % L
                slot, off, r0 = lax.rem(s0 + k, SLOTS), NB << i, c * M_BLK
                if i == 0:
                    cur = ub[pl.ds(r0, M_BLK), :]
                    if c == 0:
                        past = jnp.concatenate([e8[k], rows(hb, 0, M_BLK - NB)], axis=0).astype(BF16)
                    else:
                        past = rows(hb, r0 - NB, M_BLK).astype(BF16)
                    if c == last:
                        e8[k] = rows(hb, RB - NB, NB)
                else:
                    buf = hist[i]
                    cur = buf[k, pl.ds(off + r0, M_BLK), :]
                    past = buf[k, pl.ds(r0, M_BLK), :]
                    if c == last:
                        for r in range(0, off, RB):
                            n_rows = min(off, RB)
                            buf[k, pl.ds(r, n_rows), :] = buf[k, pl.ds(r + RB, n_rows), :]
                return preact(cur, past, slot, i)

            def g2(n, c, z):
                k, i = n // L, n % L
                un = update(z, lax.rem(s0 + k, SLOTS), i, c * M_BLK, M_BLK, hb, skb, 0)
                if i == L - 1:
                    ub[pl.ds(c * M_BLK, M_BLK), :] = un
                else:
                    hist[i + 1][k, pl.ds((NB << (i + 1)) + c * M_BLK, M_BLK), :] = un

            pipeline(block_order(count * L), g1, g2)

        def head(b, carry):
            load_block(b)
            block_stacks(0, 1)
            store_block(b)

            @pl.when((b == 0) & odd)
            def _():
                send_x_far()

            return carry

        def tail(b, carry):
            fetch_block(b)
            block_stacks(S - TAIL, TAIL)
            send_block(b)
            return carry

        clear_history()
        wait_weights(0)
        for s in range(1, SLOTS):
            start_weights(s)
        lax.fori_loop(0, G, head, 0)
        lax.fori_loop(1, S - TAIL, wide_stack, 0)
        clear_history()
        for k in range(TAIL):
            wait_weights(S - TAIL + k)
        lax.fori_loop(0, G, tail, 0)

        for o in range(1, G):
            x_remote(o, me).wait_send()
        for b in range(G - 2, G):
            sent(b)
        for b in range(G):
            for q in range(2):
                for o in range(1, G):
                    out_remote(b, q, o, lax.rem(me + G - o, G)).wait_recv()

    def local(x, wc, wp, wr, ws):
        batch, seq_blk, C = x.shape
        S, L = wc.shape[0], wc.shape[1]
        NB = batch // G
        RB = seq_blk * NB
        R = RB * G
        hist = [pltpu.VMEM((TAIL, (NB << i) + RB, C), BF16) for i in range(1, L)]
        hbm = pl.BlockSpec(memory_space=pltpu.HBM)
        out = jax.ShapeDtypeStruct((batch, 1, seq_blk, C), F32)
        return pl.pallas_call(
            kernel,
            out_shape=[out, out],
            in_specs=[hbm] * 5,
            out_specs=[pl.BlockSpec(memory_space=pl.ANY)] * 2,
            scratch_shapes=[
                pltpu.VMEM((2, R + NB, C // 2), F32),
                pltpu.VMEM((2, R, C // 2), F32),
                pltpu.VMEM((2, R + M_WIDE // 2, C), BF16),
                pltpu.VMEM((SLOTS, L, C, 2 * C), BF16),
                pltpu.VMEM((SLOTS, L, C, 2 * C), BF16),
                pltpu.VMEM((SLOTS, L, C, C), BF16),
                pltpu.VMEM((SLOTS, L, C, C), BF16),
                *hist,
                pltpu.VMEM((TAIL, NB, C), F32),
                pltpu.VMEM((2, RB, C // 2), F32),
                pltpu.VMEM((2, RB, C // 2), F32),
                pltpu.VMEM((RB, C), BF16),
                pltpu.VMEM((G, NB, seq_blk, C), BF16),
                pltpu.VMEM((2, 2, G, NB, seq_blk // G, C), F32),
                pltpu.SemaphoreType.DMA((SLOTS, 4)),
                pltpu.SemaphoreType.DMA((G,)),
                pltpu.SemaphoreType.DMA((G,)),
                pltpu.SemaphoreType.DMA,
                pltpu.SemaphoreType.DMA((G, 2, G)),
                pltpu.SemaphoreType.DMA((G, 2, G)),
                pltpu.SemaphoreType.DMA((G, 2)),
            ],
            compiler_params=pltpu.CompilerParams(collective_id=0, has_side_effects=True, vmem_limit_bytes=VMEM),
            name="stack",
        )(x, wc, wp, wr, ws)

    return jax.shard_map(local, mesh=mesh, in_specs=(P("dp", "sp", None), P(), P(), P(), P()), out_specs=(P("dp", "sp", None, None), P("dp", "sp", None, None)), check_vma=False)
```

time: 251 us -> 246 us (0.980)
  Pallas kernels: 244 us -> 241 us
    unnamed x2 -> x4, local copies, waits for them, and re-layouts: 6.26 us -> 3.86 us
where the time goes in v2:
time: 246 us
  Pallas kernels  241 us (98%)
  local copies, waits for them, and re-layouts  3.86 us (2%)
    pallas_call x1, Pallas kernels, local(): pl.pallas_call(kernel, out_shape=[out, out], in_specs=[hbm] * 5, out_spec...  241 us

profile of v2, /device:TPU:1, one launch (start us, length us, event | category | flops | bytes accessed | tf_op | source)
XLA Modules:
  0.0 245.7 jit_solution(8308739067947083784)
XLA Ops:
  0.6 0.0 copy-start
  0.6 1.2 copy-done
  1.9 241.2 %stack.1 = (f32[32,1,64,256]{3,2,1,0:T(8,128)S(1)}, f32[32,1,64,256]{3,2,1,0:T(8,128)S(1)}) custom-call(bf16[32,64,256]{2,1,0:T(8,128)(2,1)S(1)} %copy-done, bf16[16,8,256,512]{3,2,1,0:T(8,128)(2,1)} %wc.1, bf16[16,8,256,512]{3,2,1,0:T(8,128)(2,1)} %wp.1, bf16[16,8,256,256]{3,2,1,0:T(8,128)(2,1)} %wr.1, bf16[16,8,256,256]{3,2,1,0:T(8,128)(2,1)} %ws.1), custom_call_target="tpu_custom_call" | custom-call | tf_op jit(solution)/shard_map/stack/pallas_call | solution.py:293
  243.1 1.3 copy.9
  244.4 1.3 copy.10
Async XLA Ops:
  0.6 1.2 copy-start
